TPU v7x, 32 devices: a whole 2x2x4 slice. The times are simulated.
32 devices in a mesh: ctx: 8 (over y, x, core), rec: 4 (over z).
Axes of the slice: x: 2, y: 2, z: 4, core: 2. Of those that a mesh axis runs over, the one named last changes fastest.
Arguments:
- queries: bfloat16 [4, 1024, 4096], P('rec', 'ctx'), may hold values from -6 to 6
- out_grads: bfloat16 [4, 1024, 4096], P('rec', 'ctx'), may hold values from -6 to 6
- log_sums: float32 [4, 32, 1024], P('rec', None, 'ctx'), may hold values from 1.5 to 4
- deltas: float32 [4, 32, 1024], P('rec', None, 'ctx'), may hold values from -6 to 6
- keys: bfloat16 [1024, 256], P('ctx'), may hold values from -6 to 6
- values: bfloat16 [1024, 256], P('ctx'), may hold values from -0.5 to 0.5
- doc_ids: int32 [4, 8], P('rec'), may hold values from 0 to 3, never falling along the last dimension, each value on 1 to 4 neighbouring positions
Outputs:
- query_grads: bfloat16 [4, 1024, 4096], P('rec', 'ctx')
- key_grads: bfloat16 [1024, 256], P(('ctx', 'rec'))
- value_grads: bfloat16 [1024, 256], P(('ctx', 'rec'))
Inputs may be any that keep to these rules, and one draw needn't show every extreme that they name: `doc_ids`: in each row the numbers never fall, start at 0, each document spans 1 to 4 blocks and some document spans exactly 4 blocks.
All inputs are finite; a program needn't handle non-finite values.
Results may differ from a plain program's by a relative error of at most 0.0062.
Values may be sent and summed in bfloat16 or wider, within the bound.
A program may use at most 64 MiB of HBM per device.

v0:
```python
import functools
import math

import jax
import jax.numpy as jnp
from jax import lax
from jax.experimental import pallas as pl
from jax.experimental.pallas import tpu as pltpu
from jax.sharding import PartitionSpec as P

HD = 128
MAXSPAN = 4
HEADS = 16
BACK = MAXSPAN - 1
MESH = pl.DeviceIdType.MESH
FAR = 1e30
PIECES = 4


def kernel(
    q_hbm, g_hbm, sums_hbm, delta_hbm, k_hbm, v_hbm, ids_hbm,
    dq_hbm, dk_ref, dv_ref,
    q_buf, g_buf, sums_ref, delta_ref, ids_ref, kv, key_t, ds_buf, dq_buf, acc, part, landed, total, r_send, r_land,
    load_sem, own_sem, small_sem, kv_send, kv_recv, g_send, g_recv, rec_send, rec_recv, out_sem,
):
    peers = lax.axis_size("ctx")
    recs = lax.axis_size("rec")
    mine = lax.axis_index("ctx")
    rec = lax.axis_index("rec")
    rows = q_buf.shape[0]
    key_heads = kv.shape[0]
    group = q_buf.shape[1] // (key_heads * HD)
    chunks = group // HEADS
    wide = HEADS * HD
    scale = HD ** (-0.5)
    fold = scale * math.log2(math.e)
    share = rows // recs

    def own_copy(g, which):
        source = (k_hbm, v_hbm)[which]
        return pltpu.make_async_copy(
            source.at[:, pl.ds(g * HD, HD)],
            kv.at[g, which, pl.ds(0, rows), :],
            own_sem.at[g, which],
        )

    def lanes(g, c):
        return pl.ds(pl.multiple_of((g * chunks + c) * wide, wide), wide)

    def load(g, c, which):
        source, target = ((q_hbm, q_buf), (g_hbm, g_buf))[which]
        return pltpu.make_async_copy(
            source.at[0, :, lanes(g, c)], target.at[:, lanes(g, c)], load_sem.at[g, c, which]
        )

    def out_copy(g, c):
        return pltpu.make_async_copy(
            dq_buf.at[:, lanes(g, c)], dq_hbm.at[0, :, lanes(g, c)], out_sem.at[g, c]
        )

    def kv_copy(g, k):
        return pltpu.make_async_remote_copy(
            src_ref=kv.at[g, :, pl.ds(0, rows), :],
            dst_ref=kv.at[g, :, pl.ds(k * rows, rows), :],
            send_sem=kv_send.at[g, k - 1],
            recv_sem=kv_recv.at[g, k - 1],
            device_id={"ctx": lax.rem(mine + k, peers)},
            device_id_type=MESH,
        )

    def grad_copy(g, k):
        return pltpu.make_async_remote_copy(
            src_ref=part.at[g, k - 1],
            dst_ref=landed.at[g, k - 1],
            send_sem=g_send.at[g, k - 1],
            recv_sem=g_recv.at[g, k - 1],
            device_id={"ctx": lax.rem(mine - k + peers, peers)},
            device_id_type=MESH,
        )

    def rec_copy(g, j):
        target = lax.rem(rec + j, recs)
        return pltpu.make_async_remote_copy(
            src_ref=r_send.at[g, :, pl.ds(pl.multiple_of(target * share, share), share), :],
            dst_ref=r_land.at[g, j - 1],
            send_sem=rec_send.at[g, j - 1],
            recv_sem=rec_recv.at[g, j - 1],
            device_id={"rec": target},
            device_id_type=MESH,
        )

    for g in range(key_heads):
        for which in range(2):
            own_copy(g, which).start()
    small = [
        pltpu.make_async_copy(source, target, small_sem.at[i])
        for i, (source, target) in enumerate(
            ((sums_hbm, sums_ref), (delta_hbm, delta_ref), (ids_hbm, ids_ref))
        )
    ]
    for copy in small:
        copy.start()
    for g in range(key_heads):
        for c in range(chunks):
            for which in range(2):
                load(g, c, which).start()

    barrier = pltpu.get_barrier_semaphore()
    for k in range(1, MAXSPAN):
        for other in (lax.rem(mine + k, peers), lax.rem(mine - k + peers, peers)):
            pl.semaphore_signal(barrier, inc=1, device_id={"ctx": other}, device_id_type=MESH)
    for j in range(1, recs):
        pl.semaphore_signal(
            barrier, inc=1, device_id={"rec": lax.rem(rec + j, recs)}, device_id_type=MESH
        )
    for k in range(1, MAXSPAN):
        @pl.when(mine < k)
        def _():
            kv[:, :, pl.ds(k * rows, rows), :] = jnp.zeros((key_heads, 2, rows, HD), kv.dtype)

        @pl.when(mine + k >= peers)
        def _():
            landed[:, k - 1] = jnp.zeros((key_heads, 2, rows, HD), landed.dtype)
    acc[...] = jnp.zeros_like(acc)
    pl.semaphore_wait(barrier, 2 * BACK + recs - 1)

    for g in range(key_heads):
        for which in range(2):
            own_copy(g, which).wait()
        for k in range(1, MAXSPAN):
            @pl.when(mine + k < peers)
            def _():
                kv_copy(g, k).start()

    for copy in small:
        copy.wait()
    here = ids_ref[0, mine]
    far = [jnp.float32(0.0)]
    for k in range(1, MAXSPAN):
        same = (ids_ref[0, jnp.maximum(mine - k, 0)] == here) & (mine >= k)
        far.append(jnp.where(same, 0.0, FAR).astype(jnp.float32))

    def heads_down(ref, g, c):
        first = (g * chunks + c) * HEADS
        return jnp.concatenate(
            [ref[:, pl.ds(pl.multiple_of((first + i) * HD, HD), HD)] for i in range(HEADS)], axis=0
        )

    def heads_along(ref, g, c):
        first = (g * chunks + c) * HEADS
        return jnp.concatenate([ref[0, pl.ds(first + i, 1), :] for i in range(HEADS)], axis=1)

    inner = (((1,), (1,)), ((), ()))

    def sweep(g, k):
        at = pl.ds(k * rows, rows)

        @pl.loop(0, chunks)
        def _(c):
            if k == 0:
                for which in range(2):
                    load(g, c, which).wait()
            query = heads_down(q_buf, g, c)
            grad = heads_down(g_buf, g, c)
            sums = heads_along(sums_ref, g, c) * math.log2(math.e) + far[k]
            delta = heads_along(delta_ref, g, c)
            scores = lax.dot_general(
                kv[g, 0, at, :], query, inner, preferred_element_type=jnp.float32
            )
            dprobs = lax.dot_general(
                kv[g, 1, at, :], grad, inner, preferred_element_type=jnp.float32
            )
            probs = jnp.exp2(scores * fold - sums)
            if k == 0:
                u = lax.broadcasted_iota(jnp.int32, (rows, wide), 0)
                t = lax.broadcasted_iota(jnp.int32, (rows, wide), 1) & (rows - 1)
                probs = jnp.where(u <= t, probs, 0.0)
            ds = (probs * (dprobs - delta)).astype(jnp.bfloat16)
            probs = probs.astype(jnp.bfloat16)
            ds_buf[at, lanes(g, c)] = ds
            acc[g, 0, at, :] += jnp.dot(ds, query, preferred_element_type=jnp.float32)
            acc[g, 1, at, :] += jnp.dot(probs, grad, preferred_element_type=jnp.float32)

    def query_side(g):
        @pl.loop(0, chunks)
        def _(c):
            dq = jnp.dot(
                key_t[g], ds_buf[:, lanes(g, c)], preferred_element_type=jnp.float32
            ) * scale
            for i in range(HEADS):
                at = pl.ds(pl.multiple_of(((g * chunks + c) * HEADS + i) * HD, HD), HD)
                dq_buf[:, at] = dq[:, i * rows:(i + 1) * rows].T.astype(dq_buf.dtype)
            out_copy(g, c).start()

    def turn(g, k):
        at = pl.ds(k * rows, rows)
        key_t[g, :, k * rows:(k + 1) * rows] = kv[g, 0, at, :].T

    def tile(g, k):
        @pl.when(mine >= k)
        def _():
            kv_copy(g, k).wait_recv()
        sweep(g, k)
        part[g, k - 1] = acc[g, :, k * rows:(k + 1) * rows, :].astype(part.dtype)

        @pl.when(mine >= k)
        def _():
            grad_copy(g, k).start()
        turn(g, k)

    def across(g):
        whole = acc[g, :, 0:rows, :]
        for k in range(1, MAXSPAN):
            @pl.when(mine + k < peers)
            def _():
                grad_copy(g, k).wait_recv()
        for k in range(1, MAXSPAN):
            whole = whole + landed[g, k - 1].astype(jnp.float32)
        total[g] = whole
        r_send[g] = whole.astype(r_send.dtype)
        for j in range(1, recs):
            rec_copy(g, j).start()

    def close(g):
        whole = total[g, :, pl.ds(pl.multiple_of(rec * share, share), share), :]
        for j in range(1, recs):
            rec_copy(g, j).wait_recv()
            whole = whole + r_land[g, j - 1].astype(jnp.float32)
        dk_ref[:, g * HD:(g + 1) * HD] = (whole[0] * scale).astype(dk_ref.dtype)
        dv_ref[:, g * HD:(g + 1) * HD] = whole[1].astype(dv_ref.dtype)

    last = key_heads - 1
    for g in range(key_heads):
        sweep(g, 0)
        turn(g, 0)
    for g in range(key_heads):
        order = range(1, MAXSPAN) if g < last else range(BACK, 0, -1)
        for k in order:
            tile(g, k)
    for g in range(last):
        across(g)
        query_side(g)
    across(last)
    query_side(last)
    for g in range(key_heads):
        close(g)
    for g in range(key_heads):
        for c in range(chunks):
            out_copy(g, c).wait()
        for k in range(1, MAXSPAN):
            @pl.when(mine + k < peers)
            def _():
                kv_copy(g, k).wait_send()

            @pl.when(mine >= k)
            def _():
                grad_copy(g, k).wait_send()
        for j in range(1, recs):
            rec_copy(g, j).wait_send()


def finish(dq_in, dk_in, dv_in, dq_out, dk_out, dv_out, big, dk, dv, into, out):
    pieces = big.shape[0]
    depth = big.shape[1]
    pairs = [
        (dq_in.at[0, pl.ds(i * depth, depth), :], big.at[i], dq_out.at[0, pl.ds(i * depth, depth), :])
        for i in range(pieces)
    ] + [(dk_in, dk, dk_out), (dv_in, dv, dv_out)]
    ins = [pltpu.make_async_copy(p[0], p[1], into.at[i]) for i, p in enumerate(pairs)]
    outs = [pltpu.make_async_copy(p[1], p[2], out.at[i]) for i, p in enumerate(pairs)]
    for copy in ins:
        copy.start()
    for arrived, leaving in zip(ins, outs):
        arrived.wait()
        leaving.start()
    for copy in outs:
        copy.wait()


def per_device(queries, out_grads, log_sums, deltas, keys, values, doc_ids):
    recs = lax.axis_size("rec")
    rows, width = queries.shape[1:]
    key_heads = keys.shape[1] // HD
    chunks = width // (key_heads * HD * HEADS)
    span = MAXSPAN * rows
    half = jnp.bfloat16
    dma = pltpu.SemaphoreType.DMA
    far_off = pl.BlockSpec(memory_space=pltpu.HBM)
    vmem = pl.BlockSpec(memory_space=pltpu.VMEM)
    small = (rows // recs, keys.shape[1])
    shapes = (
        jax.ShapeDtypeStruct(queries.shape, half),
        jax.ShapeDtypeStruct(small, half),
        jax.ShapeDtypeStruct(small, half),
    )
    grads = pl.pallas_call(
        kernel,
        out_shape=shapes,
        in_specs=[far_off] * 7,
        out_specs=(far_off, vmem, vmem),
        scratch_shapes=[
            pltpu.VMEM((rows, width), half),
            pltpu.VMEM((rows, width), half),
            pltpu.VMEM(log_sums.shape, jnp.float32),
            pltpu.VMEM(deltas.shape, jnp.float32),
            pltpu.SMEM(doc_ids.shape, jnp.int32),
            pltpu.VMEM((key_heads, 2, span, HD), half),
            pltpu.VMEM((key_heads, HD, span), half),
            pltpu.VMEM((span, width), half),
            pltpu.VMEM((rows, width), half),
            pltpu.VMEM((key_heads, 2, span, HD), jnp.float32),
            pltpu.VMEM((key_heads, BACK, 2, rows, HD), half),
            pltpu.VMEM((key_heads, BACK, 2, rows, HD), half),
            pltpu.VMEM((key_heads, 2, rows, HD), jnp.float32),
            pltpu.VMEM((key_heads, 2, rows, HD), half),
            pltpu.VMEM((key_heads, max(recs - 1, 1), 2, rows // recs, HD), half),
            dma((key_heads, chunks, 2)),
            dma((key_heads, 2)),
            dma((3,)),
            dma((key_heads, BACK)),
            dma((key_heads, BACK)),
            dma((key_heads, BACK)),
            dma((key_heads, BACK)),
            dma((key_heads, max(recs - 1, 1))),
            dma((key_heads, max(recs - 1, 1))),
            dma((key_heads, chunks)),
        ],
        compiler_params=pltpu.CompilerParams(
            collective_id=0, has_side_effects=True, vmem_limit_bytes=67_043_328
        ),
    )(queries, out_grads, log_sums, deltas, keys, values, doc_ids)
    return pl.pallas_call(
        finish,
        out_shape=shapes,
        in_specs=[far_off] * 3,
        out_specs=(far_off,) * 3,
        scratch_shapes=[
            pltpu.VMEM((PIECES, rows // PIECES, width), half),
            pltpu.VMEM(small, half),
            pltpu.VMEM(small, half),
            dma((PIECES + 2,)),
            dma((PIECES + 2,)),
        ],
        compiler_params=pltpu.CompilerParams(vmem_limit_bytes=67_043_328),
    )(*grads)


def solution(mesh):
    return jax.shard_map(
        per_device,
        mesh=mesh,
        in_specs=(
            P("rec", "ctx", None),
            P("rec", "ctx", None),
            P("rec", None, "ctx"),
            P("rec", None, "ctx"),
            P("ctx", None),
            P("ctx", None),
            P("rec", None),
        ),
        out_specs=(P("rec", "ctx", None), P(("ctx", "rec"), None), P(("ctx", "rec"), None)),
        check_vma=False,
    )
```

profile of v0, /device:TPU:3, one launch (start us, length us, event | category | flops | bytes accessed | tf_op | source)
XLA Modules:
  0.0 26.0 jit_solution(4974297834290976339)
XLA Ops:
  0.6 23.4 %shard_map.94 = (bf16[1,128,4096]{2,1,0:T(8,128)(2,1)}, bf16[32,256]{1,0:T(8,128)(2,1)}, bf16[32,256]{1,0:T(8,128)(2,1)}) custom-call(bf16[1,128,4096]{2,1,0:T(8,128)(2,1)} %q_hbm.1, bf16[1,128,4096]{2,1,0:T(8,128)(2,1)} %g_hbm.1, f32[1,32,128]{2,1,0:T(8,128)} %sums_hbm.1, f32[1,32,128]{2,1,0:T(8,128)} %delta_hbm.1, bf16[128,256]{1,0:T(8,128)(2,1)} %k_hbm.1, ...), custom_call_target="tpu_custom_call" | custom-call | tf_op jit(solution)/shard_map/pallas_call | solution.py:296
  24.0 2.0 %shard_map.95 = (bf16[1,128,4096]{2,1,0:T(8,128)(2,1)}, bf16[32,256]{1,0:T(8,128)(2,1)}, bf16[32,256]{1,0:T(8,128)(2,1)}) custom-call(bf16[1,128,4096]{2,1,0:T(8,128)(2,1)} %get-tuple-element.6.dq_in, bf16[32,256]{1,0:T(8,128)(2,1)} %get-tuple-element.7.dk_in, bf16[32,256]{1,0:T(8,128)(2,1)} %get-tuple-element.8.dv_in), custom_call_target="tpu_custom_call" | custom-call | tf_op jit(solution)/shard_map/pallas_call | solution.py:332
where the time goes:
time: 26.2 us; the launch traced here: 26 us
  Pallas kernels  25.4 us (97%)
  between operations  0.64 us (2%)
    pallas_call x1, Pallas kernels, per_device(): pl.pallas_call(kernel, out_shape=shapes, in_specs=[far_off] * 7, out_spec...  23.4 us
    pallas_call x1, Pallas kernels, per_device(): pl.pallas_call(finish, out_shape=shapes, in_specs=[far_off] * 3, out_spec...  2.02 us

commit v1 on v0

v1 whole, which is shorter than its diff:
```python
import math

import jax
import jax.numpy as jnp
from jax import lax
from jax.experimental import pallas as pl
from jax.experimental.pallas import tpu as pltpu
from jax.sharding import PartitionSpec as P

HD = 128
MAXSPAN = 4
HEADS = 16
BACK = MAXSPAN - 1
MESH = pl.DeviceIdType.MESH
FAR = 1e30
PIECES = 4


def kernel(
    q_hbm, g_hbm, sums_hbm, delta_hbm, k_hbm, v_hbm, ids_hbm,
    dq_ref, dk_ref, dv_ref,
    q_buf, g_buf, sums_ref, delta_ref, ids_ref, kv, key_t, ds_buf, acc, part, mate, side_land, back_land,
    direct_land, total, r_send, r_land,
    load_sem, own_sem, small_sem, hop_sem, near_sem, far_sem, pass_sem, mate_sem, side_sem, back_sem,
    direct_sem, rec_sem,
):
    peers = lax.axis_size("ctx")
    recs = lax.axis_size("rec")
    mine = lax.axis_index("ctx")
    rec = lax.axis_index("rec")
    rows = q_buf.shape[0]
    key_heads = kv.shape[0]
    group = q_buf.shape[1] // (key_heads * HD)
    chunks = group // HEADS
    wide = HEADS * HD
    scale = HD ** (-0.5)
    fold = scale * math.log2(math.e)
    share = rows // recs
    last = key_heads - 1
    odd = lax.rem(mine, 2)
    even = 1 - odd
    partner = mine + even - odd
    first_k = 1 + 2 * odd
    side_k = 3 - 2 * odd

    def slot(k):
        if isinstance(k, int):
            return pl.ds(k * rows, rows)
        return pl.ds(pl.multiple_of(k * rows, rows), rows)

    def own_copy(g, which):
        source = (k_hbm, v_hbm)[which]
        return pltpu.make_async_copy(
            source.at[:, pl.ds(g * HD, HD)], kv.at[g, which, pl.ds(0, rows), :], own_sem.at[g, which]
        )

    def lanes(g, c):
        return pl.ds(pl.multiple_of((g * chunks + c) * wide, wide), wide)

    def load(g, c, which):
        source, target = ((q_hbm, q_buf), (g_hbm, g_buf))[which]
        return pltpu.make_async_copy(
            source.at[0, :, lanes(g, c)], target.at[:, lanes(g, c)], load_sem.at[g, c, which]
        )

    def remote(source, target, sems, device):
        return pltpu.make_async_remote_copy(
            src_ref=source, dst_ref=target, send_sem=sems.at[0], recv_sem=sems.at[1],
            device_id=device, device_id_type=MESH,
        )

    def hop(g):
        return remote(kv.at[g, :, slot(0), :], kv.at[g, :, slot(2), :], hop_sem.at[g], {"ctx": lax.rem(mine + 2, peers)})

    def near(g):
        return remote(kv.at[g, :, slot(0), :], kv.at[g, :, slot(1), :], near_sem.at[g], {"ctx": partner})

    def far(g):
        return remote(kv.at[g, :, slot(0), :], kv.at[g, :, slot(3), :], far_sem.at[g], {"ctx": lax.rem(mine + 3, peers)})

    def hand(g):
        return remote(kv.at[g, :, slot(2), :], kv.at[g, :, slot(side_k), :], pass_sem.at[g], {"ctx": partner})

    def mate_copy(g):
        return remote(part.at[g, first_k - 1], mate.at[g], mate_sem.at[g], {"ctx": partner})

    def side_copy(g):
        return remote(part.at[g, side_k - 1], side_land.at[g], side_sem.at[g], {"ctx": lax.rem(mine - side_k + peers, peers)})

    def back_copy(g):
        return remote(part.at[g, 1], back_land.at[g], back_sem.at[g], {"ctx": lax.rem(mine - 2 + peers, peers)})

    def shares(ref, target):
        return ref.at[:, pl.ds(pl.multiple_of(target * share, share), share), :]

    def direct_copy(j):
        target = lax.rem(rec + j, recs)
        return remote(
            shares(part.at[last, 1], target), direct_land.at[j], direct_sem.at[j],
            {"ctx": lax.rem(mine - 2 + peers, peers), "rec": target},
        )

    def rec_copy(g, j):
        target = lax.rem(rec + j, recs)
        return remote(shares(r_send.at[g], target), r_land.at[g, j - 1], rec_sem.at[g, j - 1], {"rec": target})

    for g in range(key_heads):
        for which in range(2):
            own_copy(g, which).start()
    small = [
        pltpu.make_async_copy(source, target, small_sem.at[i])
        for i, (source, target) in enumerate(
            ((sums_hbm, sums_ref), (delta_hbm, delta_ref), (ids_hbm, ids_ref))
        )
    ]
    for copy in small:
        copy.start()
    for g in range(key_heads):
        for c in range(chunks):
            for which in range(2):
                load(g, c, which).start()

    barrier = pltpu.get_barrier_semaphore()
    third = lax.rem(mine + 3 * odd - 3 * even + peers, peers)
    for other in (partner, lax.rem(mine + 2, peers), lax.rem(mine - 2 + peers, peers), third):
        pl.semaphore_signal(barrier, inc=1, device_id={"ctx": other}, device_id_type=MESH)
    for j in range(1, recs):
        pl.semaphore_signal(
            barrier, inc=1, device_id={"rec": lax.rem(rec + j, recs)}, device_id_type=MESH
        )
    for k in range(1, MAXSPAN):
        @pl.when(mine < k)
        def _():
            kv[:, :, pl.ds(k * rows, rows), :] = jnp.zeros((key_heads, 2, rows, HD), kv.dtype)

    @pl.when(mine < 2)
    def _():
        mate[...] = jnp.zeros_like(mate)

    @pl.when(mine + 2 >= peers)
    def _():
        back_land[...] = jnp.zeros_like(back_land)
        direct_land[...] = jnp.zeros_like(direct_land)

    @pl.when((odd == 1) & (mine + 3 >= peers))
    def _():
        side_land[...] = jnp.zeros_like(side_land)

    acc[...] = jnp.zeros_like(acc)
    pl.semaphore_wait(barrier, 4 + recs - 1)

    for g in range(key_heads):
        for which in range(2):
            own_copy(g, which).wait()

        @pl.when(mine + 2 < peers)
        def _():
            hop(g).start()

        @pl.when(even == 1)
        def _():
            near(g).start()

        @pl.when((odd == 1) & (mine + 3 < peers))
        def _():
            far(g).start()

    for copy in small:
        copy.wait()
    here = ids_ref[0, mine]

    def away(k):
        if isinstance(k, int) and k == 0:
            return jnp.float32(0.0)
        same = (ids_ref[0, jnp.maximum(mine - k, 0)] == here) & (mine >= k)
        return jnp.where(same, 0.0, FAR).astype(jnp.float32)

    def heads_down(ref, g, c):
        first = (g * chunks + c) * HEADS
        return jnp.concatenate(
            [ref[:, pl.ds(pl.multiple_of((first + i) * HD, HD), HD)] for i in range(HEADS)], axis=0
        )

    def heads_along(ref, g, c):
        first = (g * chunks + c) * HEADS
        return jnp.concatenate([ref[0, pl.ds(first + i, 1), :] for i in range(HEADS)], axis=1)

    inner = (((1,), (1,)), ((), ()))

    def sweep(g, k):
        at = slot(k)
        own = isinstance(k, int) and k == 0
        shift = away(k)

        @pl.loop(0, chunks)
        def _(c):
            if own:
                for which in range(2):
                    load(g, c, which).wait()
            query = heads_down(q_buf, g, c)
            grad = heads_down(g_buf, g, c)
            sums = heads_along(sums_ref, g, c) * math.log2(math.e) + shift
            delta = heads_along(delta_ref, g, c)
            scores = lax.dot_general(
                kv[g, 0, at, :], query, inner, preferred_element_type=jnp.float32
            )
            dprobs = lax.dot_general(
                kv[g, 1, at, :], grad, inner, preferred_element_type=jnp.float32
            )
            probs = jnp.exp2(scores * fold - sums)
            if own:
                u = lax.broadcasted_iota(jnp.int32, (rows, wide), 0)
                t = lax.broadcasted_iota(jnp.int32, (rows, wide), 1) & (rows - 1)
                probs = jnp.where(u <= t, probs, 0.0)
            ds = (probs * (dprobs - delta)).astype(jnp.bfloat16)
            probs = probs.astype(jnp.bfloat16)
            ds_buf[at, lanes(g, c)] = ds
            acc[g, 0, at, :] += jnp.dot(ds, query, preferred_element_type=jnp.float32)
            acc[g, 1, at, :] += jnp.dot(probs, grad, preferred_element_type=jnp.float32)

        key_t[g, :, slot(k)] = kv[g, 0, at, :].T

    def query_side(g):
        @pl.loop(0, chunks)
        def _(c):
            dq = jnp.dot(
                key_t[g], ds_buf[:, lanes(g, c)], preferred_element_type=jnp.float32
            ) * scale
            for i in range(HEADS):
                at = pl.ds(pl.multiple_of(((g * chunks + c) * HEADS + i) * HD, HD), HD)
                dq_ref[0, :, at] = dq[:, i * rows:(i + 1) * rows].T.astype(dq_ref.dtype)

    def keep(g, k):
        part[g, k - 1] = acc[g, :, slot(k), :].astype(part.dtype)

    def arrive(g):
        @pl.when(mine >= 2)
        def _():
            hop(g).wait_recv()
            hand(g).start()

    def combine(g):
        @pl.when(mine >= 2)
        def _():
            mate_copy(g).wait_recv()
        part[g, 1] = (acc[g, :, slot(2), :] + mate[g].astype(jnp.float32)).astype(part.dtype)

        @pl.when(mine >= 2)
        def _():
            if g == last:
                for j in range(recs):
                    direct_copy(j).start()
            else:
                back_copy(g).start()

    def send_mate(g):
        keep(g, first_k)

        @pl.when(mine >= 2)
        def _():
            mate_copy(g).start()

    def send_side(g):
        keep(g, side_k)

        @pl.when(mine >= side_k)
        def _():
            side_copy(g).start()

    def wait_far(g):
        @pl.when((even == 1) & (mine >= 3))
        def _():
            far(g).wait_recv()

    def wait_near(g):
        @pl.when(odd == 1)
        def _():
            near(g).wait_recv()

    def wait_hand(g):
        @pl.when(mine >= 2)
        def _():
            hand(g).wait_recv()

    def across(g):
        whole = acc[g, :, 0:rows, :]

        @pl.when((even == 1) | (mine + 3 < peers))
        def _():
            side_copy(g).wait_recv()
        whole = whole + side_land[g].astype(jnp.float32)
        if g != last:
            @pl.when(mine + 2 < peers)
            def _():
                back_copy(g).wait_recv()
            whole = whole + back_land[g].astype(jnp.float32)
        total[g] = whole
        r_send[g] = whole.astype(r_send.dtype)
        for j in range(1, recs):
            rec_copy(g, j).start()

    def close(g):
        whole = total[g, :, pl.ds(pl.multiple_of(rec * share, share), share), :]
        for j in range(1, recs):
            rec_copy(g, j).wait_recv()
            whole = whole + r_land[g, j - 1].astype(jnp.float32)
        if g == last:
            @pl.when(mine + 2 < peers)
            def _():
                for j in range(recs):
                    direct_copy(j).wait_recv()
            for j in range(recs):
                whole = whole + direct_land[j].astype(jnp.float32)
        dk_ref[:, g * HD:(g + 1) * HD] = (whole[0] * scale).astype(dk_ref.dtype)
        dv_ref[:, g * HD:(g + 1) * HD] = whole[1].astype(dv_ref.dtype)

    for g in range(key_heads):
        sweep(g, 0)
    arrive(0)
    for g in range(key_heads):
        if g == 0:
            wait_near(g)
            sweep(g, 2 - odd)
            if g < last:
                arrive(g + 1)
            wait_far(g)
            sweep(g, 3 - odd)
            send_side(g)
            wait_hand(g)
            sweep(g, first_k)
            send_mate(g)
        else:
            wait_near(g)
            wait_hand(g)
            sweep(g, first_k)
            send_mate(g)
            combine(g - 1)
            if g < last:
                arrive(g + 1)
            wait_far(g)
            sweep(g, side_k)
            send_side(g)
            sweep(g, 2)
    combine(last)
    for g in range(last):
        across(g)
        query_side(g)
    across(last)
    query_side(last)
    for g in range(key_heads):
        close(g)
    for g in range(key_heads):
        @pl.when(mine + 2 < peers)
        def _():
            hop(g).wait_send()

        @pl.when(even == 1)
        def _():
            near(g).wait_send()

        @pl.when((odd == 1) & (mine + 3 < peers))
        def _():
            far(g).wait_send()

        @pl.when(mine >= 2)
        def _():
            hand(g).wait_send()
            mate_copy(g).wait_send()
            if g == last:
                for j in range(recs):
                    direct_copy(j).wait_send()
            else:
                back_copy(g).wait_send()

        @pl.when(mine >= side_k)
        def _():
            side_copy(g).wait_send()
        for j in range(1, recs):
            rec_copy(g, j).wait_send()


def finish(dq_in, dk_in, dv_in, dq_out, dk_out, dv_out, out):
    depth = dq_in.shape[1] // PIECES
    pairs = [
        (dq_in.at[0, pl.ds(i * depth, depth), :], dq_out.at[0, pl.ds(i * depth, depth), :])
        for i in range(PIECES)
    ] + [(dk_in, dk_out), (dv_in, dv_out)]
    outs = [pltpu.make_async_copy(p[0], p[1], out.at[i]) for i, p in enumerate(pairs)]
    for copy in outs:
        copy.start()
    for copy in outs:
        copy.wait()


def per_device(queries, out_grads, log_sums, deltas, keys, values, doc_ids):
    recs = lax.axis_size("rec")
    rows, width = queries.shape[1:]
    key_heads = keys.shape[1] // HD
    chunks = width // (key_heads * HD * HEADS)
    span = MAXSPAN * rows
    half = jnp.bfloat16
    dma = pltpu.SemaphoreType.DMA
    far_off = pl.BlockSpec(memory_space=pltpu.HBM)
    vmem = pl.BlockSpec(memory_space=pltpu.VMEM)
    small = (rows // recs, keys.shape[1])
    shapes = (
        jax.ShapeDtypeStruct(queries.shape, half),
        jax.ShapeDtypeStruct(small, half),
        jax.ShapeDtypeStruct(small, half),
    )
    pair = (key_heads, 2, rows, HD)
    grads = pl.pallas_call(
        kernel,
        out_shape=shapes,
        in_specs=[far_off] * 7,
        out_specs=(vmem, vmem, vmem),
        scratch_shapes=[
            pltpu.VMEM((rows, width), half),
            pltpu.VMEM((rows, width), half),
            pltpu.VMEM(log_sums.shape, jnp.float32),
            pltpu.VMEM(deltas.shape, jnp.float32),
            pltpu.SMEM(doc_ids.shape, jnp.int32),
            pltpu.VMEM((key_heads, 2, span, HD), half),
            pltpu.VMEM((key_heads, HD, span), half),
            pltpu.VMEM((span, width), half),
            pltpu.VMEM((key_heads, 2, span, HD), jnp.float32),
            pltpu.VMEM((key_heads, BACK, 2, rows, HD), half),
            pltpu.VMEM(pair, half),
            pltpu.VMEM(pair, half),
            pltpu.VMEM(pair, half),
            pltpu.VMEM((recs, 2, rows // recs, HD), half),
            pltpu.VMEM(pair, jnp.float32),
            pltpu.VMEM(pair, half),
            pltpu.VMEM((key_heads, max(recs - 1, 1), 2, rows // recs, HD), half),
            dma((key_heads, chunks, 2)),
            dma((key_heads, 2)),
            dma((3,)),
            dma((key_heads, 2)),
            dma((key_heads, 2)),
            dma((key_heads, 2)),
            dma((key_heads, 2)),
            dma((key_heads, 2)),
            dma((key_heads, 2)),
            dma((key_heads, 2)),
            dma((recs, 2)),
            dma((key_heads, max(recs - 1, 1), 2)),
        ],
        compiler_params=pltpu.CompilerParams(
            collective_id=0, has_side_effects=True, vmem_limit_bytes=40 * 2**20
        ),
    )(*[
        pltpu.with_memory_space_constraint(x, pltpu.HBM)
        for x in (queries, out_grads, log_sums, deltas, keys, values, doc_ids)
    ])
    return pl.pallas_call(
        finish,
        out_shape=shapes,
        in_specs=[vmem] * 3,
        out_specs=(far_off,) * 3,
        scratch_shapes=[dma((PIECES + 2,))],
        compiler_params=pltpu.CompilerParams(vmem_limit_bytes=16 * 2**20),
    )(*grads)


def solution(mesh):
    return jax.shard_map(
        per_device,
        mesh=mesh,
        in_specs=(
            P("rec", "ctx", None),
            P("rec", "ctx", None),
            P("rec", None, "ctx"),
            P("rec", None, "ctx"),
            P("ctx", None),
            P("ctx", None),
            P("rec", None),
        ),
        out_specs=(P("rec", "ctx", None), P(("ctx", "rec"), None), P(("ctx", "rec"), None)),
        check_vma=False,
    )
```

time: 26.2 us -> 23 us (0.88)
  the two profiles are of different devices: /device:TPU:3 before, /device:TPU:0 now
where the time goes in v1:
time: 23 us; the launch traced here: 22.9 us
  Pallas kernels  22.2 us (97%)
  between operations  0.64 us (3%)
    pallas_call x1, Pallas kernels, per_device(): pl.pallas_call(kernel, out_shape=shapes, in_specs=[far_off] * 7, out_spec...  21.2 us
    pallas_call x1, Pallas kernels, per_device(): pl.pallas_call(finish, out_shape=shapes, in_specs=[vmem] * 3, out_specs=(...  1.02 us

profile of v1, /device:TPU:0, one launch (start us, length us, event | category | flops | bytes accessed | tf_op | source)
XLA Modules:
  0.0 22.9 jit_solution(2670845133057262187)
XLA Ops:
  0.6 21.2 %shard_map.94 = (bf16[1,128,4096]{2,1,0:T(8,128)(2,1)S(1)}, bf16[32,256]{1,0:T(8,128)(2,1)S(1)}, bf16[32,256]{1,0:T(8,128)(2,1)S(1)}) custom-call(bf16[1,128,4096]{2,1,0:T(8,128)(2,1)} %q_hbm.1, bf16[1,128,4096]{2,1,0:T(8,128)(2,1)} %g_hbm.1, f32[1,32,128]{2,1,0:T(8,128)} %sums_hbm.1, f32[1,32,128]{2,1,0:T(8,128)} %delta_hbm.1, bf16[128,256]{1,0:T(8,128)(2,1)} %k_hbm.1, ...), custom_call_target="tpu_custom_call" | custom-call | tf_op jit(solution)/shard_map/pallas_call | solution.py:412
  21.9 1.0 %shard_map.95 = (bf16[1,128,4096]{2,1,0:T(8,128)(2,1)}, bf16[32,256]{1,0:T(8,128)(2,1)}, bf16[32,256]{1,0:T(8,128)(2,1)}) custom-call(bf16[1,128,4096]{2,1,0:T(8,128)(2,1)S(1)} %get-tuple-element.6.dq_in, bf16[32,256]{1,0:T(8,128)(2,1)S(1)} %get-tuple-element.7.dk_in, bf16[32,256]{1,0:T(8,128)(2,1)S(1)} %get-tuple-element.8.dv_in), custom_call_target="tpu_custom_call" | custom-call | tf_op jit(solution)/shard_map/pallas_call | solution.py:455

commit v2 on v1

--- a/solution.py
+++ b/solution.py
@@ -19,10 +19,10 @@
 def kernel(
     q_hbm, g_hbm, sums_hbm, delta_hbm, k_hbm, v_hbm, ids_hbm,
     dq_ref, dk_ref, dv_ref,
-    q_buf, g_buf, sums_ref, delta_ref, ids_ref, kv, key_t, ds_buf, acc, part, mate, side_land, back_land,
-    direct_land, total, r_send, r_land,
-    load_sem, own_sem, small_sem, hop_sem, near_sem, far_sem, pass_sem, mate_sem, side_sem, back_sem,
-    direct_sem, rec_sem,
+    q_buf, g_buf, sums_ref, delta_ref, ids_ref, kv, key_t, ds_buf, acc, part, mate, side_land,
+    direct_land, skip_land, total, r_send, r_land,
+    load_sem, own_sem, small_sem, hop_sem, near_sem, far_sem, pass_sem, mate_sem, side_sem,
+    direct_sem, skip_sem, rec_sem, ready_sem,
 ):
     peers = lax.axis_size("ctx")
     recs = lax.axis_size("rec")
@@ -69,14 +69,17 @@
             device_id=device, device_id_type=MESH,
         )
 
+    def ship(g, k, sems, device):
+        return [remote(kv.at[g, :, slot(0), :], kv.at[g, :, slot(k), :], sems.at[g], {"ctx": device})]
+
     def hop(g):
-        return remote(kv.at[g, :, slot(0), :], kv.at[g, :, slot(2), :], hop_sem.at[g], {"ctx": lax.rem(mine + 2, peers)})
+        return ship(g, 2, hop_sem, lax.rem(mine + 2, peers))
 
     def near(g):
-        return remote(kv.at[g, :, slot(0), :], kv.at[g, :, slot(1), :], near_sem.at[g], {"ctx": partner})
+        return ship(g, 1, near_sem, partner)
 
     def far(g):
-        return remote(kv.at[g, :, slot(0), :], kv.at[g, :, slot(3), :], far_sem.at[g], {"ctx": lax.rem(mine + 3, peers)})
+        return ship(g, 3, far_sem, lax.rem(mine + 3, peers))
 
     def hand(g):
         return remote(kv.at[g, :, slot(2), :], kv.at[g, :, slot(side_k), :], pass_sem.at[g], {"ctx": partner})
@@ -85,24 +88,60 @@
         return remote(part.at[g, first_k - 1], mate.at[g], mate_sem.at[g], {"ctx": partner})
 
     def side_copy(g):
-        return remote(part.at[g, side_k - 1], side_land.at[g], side_sem.at[g], {"ctx": lax.rem(mine - side_k + peers, peers)})
-
-    def back_copy(g):
-        return remote(part.at[g, 1], back_land.at[g], back_sem.at[g], {"ctx": lax.rem(mine - 2 + peers, peers)})
+        return remote(part.at[g, 0], side_land.at[g], side_sem.at[g], {"ctx": partner})
 
     def shares(ref, target):
         return ref.at[:, pl.ds(pl.multiple_of(target * share, share), share), :]
 
-    def direct_copy(j):
-        target = lax.rem(rec + j, recs)
-        return remote(
-            shares(part.at[last, 1], target), direct_land.at[j], direct_sem.at[j],
-            {"ctx": lax.rem(mine - 2 + peers, peers), "rec": target},
-        )
+    def scatter(g, k, land, sems, target, slot_there):
+        return pltpu.make_async_remote_copy(
+            src_ref=shares(part.at[g, k - 1], target), dst_ref=land.at[g, slot_there],
+            send_sem=sems.at[g, target, 0], recv_sem=sems.at[g, slot_there, 1],
+            device_id={"ctx": lax.rem(mine - k + peers, peers), "rec": target}, device_id_type=MESH,
+        )
+
+    def direct_copy(g, target):
+        return scatter(g, 2, direct_land, direct_sem, target, rec)
+
+    def skip_copy(g, target):
+        return scatter(g, 3, skip_land, skip_sem, target, rec)
+
+    def direct_from(g, source):
+        return scatter(g, 2, direct_land, direct_sem, source, source)
+
+    def skip_from(g, source):
+        return scatter(g, 3, skip_land, skip_sem, source, source)
 
     def rec_copy(g, j):
         target = lax.rem(rec + j, recs)
         return remote(shares(r_send.at[g], target), r_land.at[g, j - 1], rec_sem.at[g, j - 1], {"rec": target})
+
+    barrier = pltpu.get_barrier_semaphore()
+    third = mine + 3 * odd - 3 * even
+    greeted = jnp.int32(recs - 1)
+    for other in (partner, mine + 2, mine - 2, third):
+        there = (other >= 0) & (other < peers)
+        greeted = greeted + jnp.where(there, 1, 0)
+
+        @pl.when(there)
+        def _():
+            pl.semaphore_signal(barrier, inc=1, device_id={"ctx": other}, device_id_type=MESH)
+    for j in range(1, recs):
+        pl.semaphore_signal(
+            barrier, inc=1, device_id={"rec": lax.rem(rec + j, recs)}, device_id_type=MESH
+        )
+
+    def begin(copies):
+        for copy in copies:
+            copy.start()
+
+    def landed(copies):
+        for copy in copies:
+            copy.wait_recv()
+
+    def sent(copies):
+        for copy in copies:
+            copy.wait_send()
 
     for g in range(key_heads):
         for which in range(2):
@@ -120,14 +159,6 @@
             for which in range(2):
                 load(g, c, which).start()
 
-    barrier = pltpu.get_barrier_semaphore()
-    third = lax.rem(mine + 3 * odd - 3 * even + peers, peers)
-    for other in (partner, lax.rem(mine + 2, peers), lax.rem(mine - 2 + peers, peers), third):
-        pl.semaphore_signal(barrier, inc=1, device_id={"ctx": other}, device_id_type=MESH)
-    for j in range(1, recs):
-        pl.semaphore_signal(
-            barrier, inc=1, device_id={"rec": lax.rem(rec + j, recs)}, device_id_type=MESH
-        )
     for k in range(1, MAXSPAN):
         @pl.when(mine < k)
         def _():
@@ -139,15 +170,18 @@
 
     @pl.when(mine + 2 >= peers)
     def _():
-        back_land[...] = jnp.zeros_like(back_land)
         direct_land[...] = jnp.zeros_like(direct_land)
 
-    @pl.when((odd == 1) & (mine + 3 >= peers))
+    @pl.when((even == 1) | (mine + 3 >= peers))
     def _():
-        side_land[...] = jnp.zeros_like(side_land)
+        skip_land[...] = jnp.zeros_like(skip_land)
 
     acc[...] = jnp.zeros_like(acc)
-    pl.semaphore_wait(barrier, 4 + recs - 1)
+    pl.semaphore_wait(barrier, greeted)
+    for j in range(1, recs):
+        pl.semaphore_signal(
+            ready_sem, inc=1, device_id={"rec": lax.rem(rec + j, recs)}, device_id_type=MESH
+        )
 
     for g in range(key_heads):
         for which in range(2):
@@ -155,15 +189,11 @@
 
         @pl.when(mine + 2 < peers)
         def _():
-            hop(g).start()
+            begin(hop(g))
 
         @pl.when(even == 1)
         def _():
-            near(g).start()
-
-        @pl.when((odd == 1) & (mine + 3 < peers))
-        def _():
-            far(g).start()
+            begin(near(g))
 
     for copy in small:
         copy.wait()
@@ -236,22 +266,20 @@
     def arrive(g):
         @pl.when(mine >= 2)
         def _():
-            hop(g).wait_recv()
+            landed(hop(g))
             hand(g).start()
 
     def combine(g):
         @pl.when(mine >= 2)
         def _():
             mate_copy(g).wait_recv()
-        part[g, 1] = (acc[g, :, slot(2), :] + mate[g].astype(jnp.float32)).astype(part.dtype)
+        whole = acc[g, :, slot(2), :] + mate[g].astype(jnp.float32)
+        part[g, 1] = whole.astype(part.dtype)
 
         @pl.when(mine >= 2)
         def _():
-            if g == last:
-                for j in range(recs):
-                    direct_copy(j).start()
-            else:
-                back_copy(g).start()
+            for j in range(recs):
+                direct_copy(g, j).start()
 
     def send_mate(g):
         keep(g, first_k)
@@ -260,40 +288,29 @@
         def _():
             mate_copy(g).start()
 
-    def send_side(g):
-        keep(g, side_k)
-
-        @pl.when(mine >= side_k)
-        def _():
-            side_copy(g).start()
+    def send_skip(g):
+        keep(g, 3)
+
+        @pl.when(mine >= 3)
+        def _():
+            for j in range(recs):
+                skip_copy(g, j).start()
 
     def wait_far(g):
-        @pl.when((even == 1) & (mine >= 3))
-        def _():
-            far(g).wait_recv()
-
-    def wait_near(g):
-        @pl.when(odd == 1)
-        def _():
-            near(g).wait_recv()
+        @pl.when(mine >= 3)
+        def _():
+            landed(far(g))
 
     def wait_hand(g):
         @pl.when(mine >= 2)
         def _():
             hand(g).wait_recv()
 
-    def across(g):
+    def across(g, with_side):
         whole = acc[g, :, 0:rows, :]
-
-        @pl.when((even == 1) | (mine + 3 < peers))
-        def _():
+        if with_side:
             side_copy(g).wait_recv()
-        whole = whole + side_land[g].astype(jnp.float32)
-        if g != last:
-            @pl.when(mine + 2 < peers)
-            def _():
-                back_copy(g).wait_recv()
-            whole = whole + back_land[g].astype(jnp.float32)
+            whole = whole + side_land[g].astype(jnp.float32)
         total[g] = whole
         r_send[g] = whole.astype(r_send.dtype)
         for j in range(1, recs):
@@ -304,77 +321,104 @@
         for j in range(1, recs):
             rec_copy(g, j).wait_recv()
             whole = whole + r_land[g, j - 1].astype(jnp.float32)
-        if g == last:
-            @pl.when(mine + 2 < peers)
-            def _():
-                for j in range(recs):
-                    direct_copy(j).wait_recv()
+
+        @pl.when(mine + 2 < peers)
+        def _():
             for j in range(recs):
-                whole = whole + direct_land[j].astype(jnp.float32)
+                direct_from(g, j).wait_recv()
+
+        @pl.when((odd == 1) & (mine + 3 < peers))
+        def _():
+            for j in range(recs):
+                skip_from(g, j).wait_recv()
+        for j in range(recs):
+            whole = whole + direct_land[g, j].astype(jnp.float32) + skip_land[g, j].astype(jnp.float32)
         dk_ref[:, g * HD:(g + 1) * HD] = (whole[0] * scale).astype(dk_ref.dtype)
         dv_ref[:, g * HD:(g + 1) * HD] = whole[1].astype(dv_ref.dtype)
 
     for g in range(key_heads):
         sweep(g, 0)
+
+    @pl.when(odd == 1)
+    def _():
+        for g in range(key_heads):
+            across(g, False)
+        for g in range(key_heads):
+            landed(near(g))
+            sweep(g, 1)
+            keep(g, 1)
+            side_copy(g).start()
+            if g == 0:
+                @pl.when(mine + 3 < peers)
+                def _():
+                    for h in range(key_heads):
+                        begin(far(h))
+
     arrive(0)
-    for g in range(key_heads):
-        if g == 0:
-            wait_near(g)
-            sweep(g, 2 - odd)
-            if g < last:
-                arrive(g + 1)
+    sweep(0, 2)
+    for g in range(1, key_heads):
+        arrive(g)
+    wait_hand(0)
+    sweep(0, first_k)
+    send_mate(0)
+    pl.semaphore_wait(ready_sem, recs - 1)
+
+    @pl.when(even == 1)
+    def _():
+        for g in range(key_heads):
+            across(g, True)
+        for g in range(key_heads):
+            if g > 0:
+                wait_hand(g)
+                sweep(g, 1)
+                send_mate(g)
+                combine(g - 1)
             wait_far(g)
-            sweep(g, 3 - odd)
-            send_side(g)
+            sweep(g, 3)
+            send_skip(g)
+        sweep(last, 2)
+
+    @pl.when(odd == 1)
+    def _():
+        for g in range(1, key_heads):
+            sweep(g, 2)
+            combine(g - 1)
             wait_hand(g)
-            sweep(g, first_k)
+            sweep(g, 3)
             send_mate(g)
-        else:
-            wait_near(g)
-            wait_hand(g)
-            sweep(g, first_k)
-            send_mate(g)
-            combine(g - 1)
-            if g < last:
-                arrive(g + 1)
-            wait_far(g)
-            sweep(g, side_k)
-            send_side(g)
-            sweep(g, 2)
     combine(last)
-    for g in range(last):
-        across(g)
+    for g in range(key_heads):
         query_side(g)
-    across(last)
-    query_side(last)
     for g in range(key_heads):
         close(g)
     for g in range(key_heads):
         @pl.when(mine + 2 < peers)
         def _():
-            hop(g).wait_send()
+            sent(hop(g))
 
         @pl.when(even == 1)
         def _():
-            near(g).wait_send()
+            sent(near(g))
 
         @pl.when((odd == 1) & (mine + 3 < peers))
         def _():
-            far(g).wait_send()
+            sent(far(g))
 
         @pl.when(mine >= 2)
         def _():
             hand(g).wait_send()
             mate_copy(g).wait_send()
-            if g == last:
-                for j in range(recs):
-                    direct_copy(j).wait_send()
-            else:
-                back_copy(g).wait_send()
-
-        @pl.when(mine >= side_k)
+            for j in range(recs):
+                direct_copy(g, j).wait_send()
+
+        @pl.when(odd == 1)
         def _():
             side_copy(g).wait_send()
+
+        @pl.when((even == 1) & (mine >= 3))
+        def _():
+            for j in range(recs):
+                skip_copy(g, j).wait_send()
         for j in range(1, recs):
             rec_copy(g, j).wait_send()
 
@@ -427,8 +471,8 @@
             pltpu.VMEM((key_heads, BACK, 2, rows, HD), half),
             pltpu.VMEM(pair, half),
             pltpu.VMEM(pair, half),
-            pltpu.VMEM(pair, half),
-            pltpu.VMEM((recs, 2, rows // recs, HD), half),
+            pltpu.VMEM((key_heads, recs, 2, rows // recs, HD), half),
+            pltpu.VMEM((key_heads, recs, 2, rows // recs, HD), half),
             pltpu.VMEM(pair, jnp.float32),
             pltpu.VMEM(pair, half),
             pltpu.VMEM((key_heads, max(recs - 1, 1), 2, rows // recs, HD), half),
@@ -441,9 +485,10 @@
             dma((key_heads, 2)),
             dma((key_heads, 2)),
             dma((key_heads, 2)),
-            dma((key_heads, 2)),
-            dma((recs, 2)),
+            dma((key_heads, recs, 2)),
+            dma((key_heads, recs, 2)),
             dma((key_heads, max(recs - 1, 1), 2)),
+            pltpu.SemaphoreType.REGULAR,
         ],
         compiler_params=pltpu.CompilerParams(
             collective_id=0, has_side_effects=True, vmem_limit_bytes=40 * 2**20

time: 23 us -> 21.3 us (0.926)
  the two profiles are of different devices: /device:TPU:0 before, /device:TPU:1 now
where the time goes in v2:
time: 21.3 us; the launch traced here: 21.1 us
  Pallas kernels  20.5 us (96%)
  between operations  0.64 us (3%)
    pallas_call x1, Pallas kernels, per_device(): pl.pallas_call(kernel, out_shape=shapes, in_specs=[far_off] * 7, out_spec...  19.5 us
    pallas_call x1, Pallas kernels, per_device(): pl.pallas_call(finish, out_shape=shapes, in_specs=[vmem] * 3, out_specs=(...  1.02 us

profile of v2, /device:TPU:1, one launch (start us, length us, event | category | flops | bytes accessed | tf_op | source)
XLA Modules:
  0.0 21.1 jit_solution(14427754221593699712)
XLA Ops:
  0.6 19.5 %shard_map.94 = (bf16[1,128,4096]{2,1,0:T(8,128)(2,1)S(1)}, bf16[32,256]{1,0:T(8,128)(2,1)S(1)}, bf16[32,256]{1,0:T(8,128)(2,1)S(1)}) custom-call(bf16[1,128,4096]{2,1,0:T(8,128)(2,1)} %q_hbm.1, bf16[1,128,4096]{2,1,0:T(8,128)(2,1)} %g_hbm.1, f32[1,32,128]{2,1,0:T(8,128)} %sums_hbm.1, f32[1,32,128]{2,1,0:T(8,128)} %delta_hbm.1, bf16[128,256]{1,0:T(8,128)(2,1)} %k_hbm.1, ...), custom_call_target="tpu_custom_call" | custom-call | tf_op jit(solution)/shard_map/pallas_call | solution.py:456
  20.1 1.0 %shard_map.95 = (bf16[1,128,4096]{2,1,0:T(8,128)(2,1)}, bf16[32,256]{1,0:T(8,128)(2,1)}, bf16[32,256]{1,0:T(8,128)(2,1)}) custom-call(bf16[1,128,4096]{2,1,0:T(8,128)(2,1)S(1)} %get-tuple-element.6.dq_in, bf16[32,256]{1,0:T(8,128)(2,1)S(1)} %get-tuple-element.7.dk_in, bf16[32,256]{1,0:T(8,128)(2,1)S(1)} %get-tuple-element.8.dv_in), custom_call_target="tpu_custom_call" | custom-call | tf_op jit(solution)/shard_map/pallas_call | solution.py:500

commit v3 on v2

--- a/solution.py
+++ b/solution.py
@@ -13,7 +13,7 @@
 BACK = MAXSPAN - 1
 MESH = pl.DeviceIdType.MESH
 FAR = 1e30
-PIECES = 4
+PIECES = 1
 
 
 def kernel(
@@ -348,11 +348,11 @@
             sweep(g, 1)
             keep(g, 1)
             side_copy(g).start()
-            if g == 0:
-                @pl.when(mine + 3 < peers)
-                def _():
-                    for h in range(key_heads):
-                        begin(far(h))
+
+        @pl.when(mine + 3 < peers)
+        def _():
+            for h in range(key_heads):
+                begin(far(h))
 
     arrive(0)
     sweep(0, 2)
@@ -365,8 +365,6 @@
 
     @pl.when(even == 1)
     def _():
-        for g in range(key_heads):
-            across(g, True)
         for g in range(key_heads):
             if g > 0:
                 wait_hand(g)
@@ -377,16 +375,19 @@
             sweep(g, 3)
             send_skip(g)
         sweep(last, 2)
+        combine(last)
+        for g in range(key_heads):
+            across(g, True)
 
     @pl.when(odd == 1)
     def _():
         for g in range(1, key_heads):
-            sweep(g, 2)
             combine(g - 1)
             wait_hand(g)
             sweep(g, 3)
             send_mate(g)
-    combine(last)
+            sweep(g, 2)
+        combine(last)
     for g in range(key_heads):
         query_side(g)
     for g in range(key_heads):

time: 21.3 us -> 20.7 us (0.972)
  the two profiles are of different devices: /device:TPU:1 before, /device:TPU:4 now
where the time goes in v3:
time: 20.7 us; the launch traced here: 20.5 us
  Pallas kernels  19.9 us (96%)
  between operations  0.64 us (3%)
    pallas_call x1, Pallas kernels, per_device(): pl.pallas_call(kernel, out_shape=shapes, in_specs=[far_off] * 7, out_spec...  18.9 us
    pallas_call x1, Pallas kernels, per_device(): pl.pallas_call(finish, out_shape=shapes, in_specs=[vmem] * 3, out_specs=(...  1 us

profile of v3, /device:TPU:4, one launch (start us, length us, event | category | flops | bytes accessed | tf_op | source)
XLA Modules:
  0.0 20.5 jit_solution(745828087412809434)
XLA Ops:
  0.6 18.9 %shard_map.94 = (bf16[1,128,4096]{2,1,0:T(8,128)(2,1)S(1)}, bf16[32,256]{1,0:T(8,128)(2,1)S(1)}, bf16[32,256]{1,0:T(8,128)(2,1)S(1)}) custom-call(bf16[1,128,4096]{2,1,0:T(8,128)(2,1)} %q_hbm.1, bf16[1,128,4096]{2,1,0:T(8,128)(2,1)} %g_hbm.1, f32[1,32,128]{2,1,0:T(8,128)} %sums_hbm.1, f32[1,32,128]{2,1,0:T(8,128)} %delta_hbm.1, bf16[128,256]{1,0:T(8,128)(2,1)} %k_hbm.1, ...), custom_call_target="tpu_custom_call" | custom-call | tf_op jit(solution)/shard_map/pallas_call | solution.py:457
  19.5 1.0 %shard_map.95 = (bf16[1,128,4096]{2,1,0:T(8,128)(2,1)}, bf16[32,256]{1,0:T(8,128)(2,1)}, bf16[32,256]{1,0:T(8,128)(2,1)}) custom-call(bf16[1,128,4096]{2,1,0:T(8,128)(2,1)S(1)} %get-tuple-element.6.dq_in, bf16[32,256]{1,0:T(8,128)(2,1)S(1)} %get-tuple-element.7.dk_in, bf16[32,256]{1,0:T(8,128)(2,1)S(1)} %get-tuple-element.8.dv_in), custom_call_target="tpu_custom_call" | custom-call | tf_op jit(solution)/shard_map/pallas_call | solution.py:501

commit v4 on v3

--- a/solution.py
+++ b/solution.py
@@ -90,12 +90,12 @@
     def side_copy(g):
         return remote(part.at[g, 0], side_land.at[g], side_sem.at[g], {"ctx": partner})
 
-    def shares(ref, target):
-        return ref.at[:, pl.ds(pl.multiple_of(target * share, share), share), :]
+    def split(block):
+        return jnp.stack([block[:, t * share:(t + 1) * share, :] for t in range(recs)])
 
     def scatter(g, k, land, sems, target, slot_there):
         return pltpu.make_async_remote_copy(
-            src_ref=shares(part.at[g, k - 1], target), dst_ref=land.at[g, slot_there],
+            src_ref=part.at[g, k - 1, target], dst_ref=land.at[g, slot_there],
             send_sem=sems.at[g, target, 0], recv_sem=sems.at[g, slot_there, 1],
             device_id={"ctx": lax.rem(mine - k + peers, peers), "rec": target}, device_id_type=MESH,
         )
@@ -114,7 +114,7 @@
 
     def rec_copy(g, j):
         target = lax.rem(rec + j, recs)
-        return remote(shares(r_send.at[g], target), r_land.at[g, j - 1], rec_sem.at[g, j - 1], {"rec": target})
+        return remote(r_send.at[g, target], r_land.at[g, j - 1], rec_sem.at[g, j - 1], {"rec": target})
 
     barrier = pltpu.get_barrier_semaphore()
     third = mine + 3 * odd - 3 * even
@@ -176,7 +176,8 @@
     def _():
         skip_land[...] = jnp.zeros_like(skip_land)
 
-    acc[...] = jnp.zeros_like(acc)
+    if chunks > 1:
+        acc[...] = jnp.zeros_like(acc)
     pl.semaphore_wait(barrier, greeted)
     for j in range(1, recs):
         pl.semaphore_signal(
@@ -245,8 +246,13 @@
             ds = (probs * (dprobs - delta)).astype(jnp.bfloat16)
             probs = probs.astype(jnp.bfloat16)
             ds_buf[at, lanes(g, c)] = ds
-            acc[g, 0, at, :] += jnp.dot(ds, query, preferred_element_type=jnp.float32)
-            acc[g, 1, at, :] += jnp.dot(probs, grad, preferred_element_type=jnp.float32)
+            key_part = jnp.dot(ds, query, preferred_element_type=jnp.float32)
+            value_part = jnp.dot(probs, grad, preferred_element_type=jnp.float32)
+            if chunks > 1:
+                key_part = key_part + acc[g, 0, at, :]
+                value_part = value_part + acc[g, 1, at, :]
+            acc[g, 0, at, :] = key_part
+            acc[g, 1, at, :] = value_part
 
         key_t[g, :, slot(k)] = kv[g, 0, at, :].T
 
@@ -261,7 +267,7 @@
                 dq_ref[0, :, at] = dq[:, i * rows:(i + 1) * rows].T.astype(dq_ref.dtype)
 
     def keep(g, k):
-        part[g, k - 1] = acc[g, :, slot(k), :].astype(part.dtype)
+        part[g, k - 1] = split(acc[g, :, slot(k), :]).astype(part.dtype)
 
     def arrive(g):
         @pl.when(mine >= 2)
@@ -273,7 +279,7 @@
         @pl.when(mine >= 2)
         def _():
             mate_copy(g).wait_recv()
-        whole = acc[g, :, slot(2), :] + mate[g].astype(jnp.float32)
+        whole = split(acc[g, :, slot(2), :]) + mate[g].astype(jnp.float32)
         part[g, 1] = whole.astype(part.dtype)
 
         @pl.when(mine >= 2)
@@ -307,7 +313,7 @@
             hand(g).wait_recv()
 
     def across(g, with_side):
-        whole = acc[g, :, 0:rows, :]
+        whole = split(acc[g, :, 0:rows, :])
         if with_side:
             side_copy(g).wait_recv()
             whole = whole + side_land[g].astype(jnp.float32)
@@ -317,7 +323,7 @@
             rec_copy(g, j).start()
 
     def close(g):
-        whole = total[g, :, pl.ds(pl.multiple_of(rec * share, share), share), :]
+        whole = total[g, rec]
         for j in range(1, recs):
             rec_copy(g, j).wait_recv()
             whole = whole + r_land[g, j - 1].astype(jnp.float32)
@@ -453,7 +459,7 @@
         jax.ShapeDtypeStruct(small, half),
         jax.ShapeDtypeStruct(small, half),
     )
-    pair = (key_heads, 2, rows, HD)
+    pair = (key_heads, recs, 2, rows // recs, HD)
     grads = pl.pallas_call(
         kernel,
         out_shape=shapes,
@@ -469,7 +475,7 @@
             pltpu.VMEM((key_heads, HD, span), half),
             pltpu.VMEM((span, width), half),
             pltpu.VMEM((key_heads, 2, span, HD), jnp.float32),
-            pltpu.VMEM((key_heads, BACK, 2, rows, HD), half),
+            pltpu.VMEM((key_heads, BACK) + pair[1:], half),
             pltpu.VMEM(pair, half),
             pltpu.VMEM(pair, half),
             pltpu.VMEM((key_heads, recs, 2, rows // recs, HD), half),

time: 20.7 us -> 20.7 us (level)
  no operation moved by 1% of the time
where the time goes in v4:
time: 20.7 us; the launch traced here: 20.5 us
  Pallas kernels  19.9 us (96%)
  between operations  0.64 us (3%)
    pallas_call x1, Pallas kernels, per_device(): pl.pallas_call(kernel, out_shape=shapes, in_specs=[far_off] * 7, out_spec...  18.9 us
    pallas_call x1, Pallas kernels, per_device(): pl.pallas_call(finish, out_shape=shapes, in_specs=[vmem] * 3, out_specs=(...  1 us

profile of v4, /device:TPU:4, one launch (start us, length us, event | category | flops | bytes accessed | tf_op | source)
XLA Modules:
  0.0 20.5 jit_solution(9388830756540122030)
XLA Ops:
  0.6 18.9 %shard_map.94 = (bf16[1,128,4096]{2,1,0:T(8,128)(2,1)S(1)}, bf16[32,256]{1,0:T(8,128)(2,1)S(1)}, bf16[32,256]{1,0:T(8,128)(2,1)S(1)}) custom-call(bf16[1,128,4096]{2,1,0:T(8,128)(2,1)} %q_hbm.1, bf16[1,128,4096]{2,1,0:T(8,128)(2,1)} %g_hbm.1, f32[1,32,128]{2,1,0:T(8,128)} %sums_hbm.1, f32[1,32,128]{2,1,0:T(8,128)} %delta_hbm.1, bf16[128,256]{1,0:T(8,128)(2,1)} %k_hbm.1, ...), custom_call_target="tpu_custom_call" | custom-call | tf_op jit(solution)/shard_map/pallas_call | solution.py:463
  19.5 1.0 %shard_map.95 = (bf16[1,128,4096]{2,1,0:T(8,128)(2,1)}, bf16[32,256]{1,0:T(8,128)(2,1)}, bf16[32,256]{1,0:T(8,128)(2,1)}) custom-call(bf16[1,128,4096]{2,1,0:T(8,128)(2,1)S(1)} %get-tuple-element.6.dq_in, bf16[32,256]{1,0:T(8,128)(2,1)S(1)} %get-tuple-element.7.dk_in, bf16[32,256]{1,0:T(8,128)(2,1)S(1)} %get-tuple-element.8.dv_in), custom_call_target="tpu_custom_call" | custom-call | tf_op jit(solution)/shard_map/pallas_call | solution.py:507
